TPU v7x, 256 devices: a whole 4x4x8 slice. The times are simulated.
256 devices in a mesh: graph: 256 (over z, y, x, core).
Axes of the slice: x: 4, y: 4, z: 8, core: 2. Of those that a mesh axis runs over, the one named last changes fastest.
Arguments:
- feats: bfloat16 [1048576, 200], P('graph')
- w_one: float32 [200, 512], replicated
- w_two: float32 [512, 107], replicated
- send_idx: int32 [65536, 4], P('graph')
- send_count: int32 [65536], P('graph')
- edge_src: int32 [1048576, 8], P('graph')
- edge_wt: float32 [1048576, 8], P('graph')
- labels: int32 [1048576], P('graph')
- label_mask: int32 [1048576], P('graph')
Outputs:
- output 1: float32 [], replicated
- output 2: float32 [200, 512], replicated
- output 3: float32 [512, 107], replicated
All inputs are finite; a program needn't handle non-finite values.
Results may differ from a plain program's by a relative error of at most 0.001.
Values are sent between devices in bfloat16 or wider.
A program may use at most 768 MiB of HBM per device.

v0:
```python
import jax
import jax.numpy as jnp
from jax import lax
from jax.sharding import PartitionSpec as P


def solution(mesh):
    dev_count = mesh.shape["graph"]

    def device_step(feats, w_one, w_two, send_idx, send_count, edge_src, edge_wt, labels, label_mask):
        row_count = feats.shape[0]
        halo_rows = send_idx.shape[1]
        in_deg = edge_src.shape[1]
        list_ids = send_idx.reshape(dev_count * halo_rows)
        list_ok = (jnp.arange(halo_rows)[None, :] < send_count[:, None]).reshape(dev_count * halo_rows, 1)
        flat_src = edge_src.reshape(row_count * in_deg)
        w_one_b = w_one.astype(jnp.bfloat16)
        w_two_b = w_two.astype(jnp.bfloat16)

        def aggregate(h_rows):
            outgoing = jnp.where(list_ok, h_rows[list_ids], 0)
            incoming = lax.all_to_all(outgoing, "graph", 0, 0, tiled=True)
            ext_rows = jnp.concatenate([h_rows, incoming], axis=0)
            return jnp.sum(ext_rows[edge_src].astype(jnp.float32) * edge_wt[:, :, None], axis=1)

        z_one = aggregate(feats).astype(jnp.bfloat16)
        h_one = jnp.maximum(jnp.dot(z_one, w_one_b, preferred_element_type=jnp.float32), 0.0).astype(jnp.bfloat16)
        z_two = aggregate(h_one).astype(jnp.bfloat16)
        logits = jnp.dot(z_two, w_two_b, preferred_element_type=jnp.float32)
        mask_f = label_mask.astype(jnp.float32)
        label_total = lax.psum(jnp.sum(mask_f), "graph")
        log_prob = jax.nn.log_softmax(logits, axis=-1)
        onehot = (labels[:, None] == jnp.arange(logits.shape[1])[None, :]).astype(jnp.float32)
        loss_val = -lax.psum(jnp.sum(mask_f[:, None] * onehot * log_prob), "graph") / label_total
        d_logits = ((jnp.exp(log_prob) - onehot) * (mask_f / label_total)[:, None]).astype(jnp.bfloat16)
        grad_two = lax.psum(jnp.einsum("nf,nc->fc", z_two, d_logits, preferred_element_type=jnp.float32), "graph")
        d_z2 = jnp.einsum("nc,fc->nf", d_logits, w_two_b, preferred_element_type=jnp.float32)
        contrib = (edge_wt[:, :, None] * d_z2[:, None, :]).reshape(row_count * in_deg, d_z2.shape[1])
        ext_grad = jax.ops.segment_sum(contrib, flat_src, num_segments=row_count + dev_count * halo_rows)
        returned = lax.all_to_all(ext_grad[row_count:], "graph", 0, 0, tiled=True)
        d_h1 = ext_grad[:row_count] + jax.ops.segment_sum(jnp.where(list_ok, returned, 0.0), list_ids, num_segments=row_count)
        d_y1 = jnp.where(h_one > 0, d_h1, 0.0).astype(jnp.bfloat16)
        grad_one = lax.psum(jnp.einsum("nf,nh->fh", z_one, d_y1, preferred_element_type=jnp.float32), "graph")
        return loss_val, grad_one, grad_two

    row_spec = P("graph", None)
    vec_spec = P("graph")
    return jax.shard_map(device_step, mesh=mesh, in_specs=(row_spec, P(), P(), row_spec, vec_spec, row_spec, row_spec, vec_spec, vec_spec), out_specs=(P(), P(), P()), check_vma=False)
```

profile of v0, /device:TPU:2, one launch (start us, length us, event | category | flops | bytes accessed | tf_op | source)
XLA Modules:
  0.0 1078.4 jit_solution(14435136427846695725)
XLA Ops:
  8.7 3.2 copy.18
  11.8 3.9 gather_fusion
  17.3 14.7 %all-to-all-start = ((bf16[256,4,200]{2,1,0:T(4,128)(2,1)}), bf16[256,4,200]{2,1,0:T(4,128)(2,1)S(1)}, u32[]{:S(2)}, u32[]{:S(2)}) async-start(bf16[256,4,200]{2,1,0:T(4,128)(2,1)} %broadcast_select_fusion.1), calls=%async_computation | async-start | bytes 1048576 | tf_op jit(solution)/shard_map/all_to_all | solution.py:22
  35.7 15.5 %all-to-all-done = bf16[256,4,200]{2,1,0:T(4,128)(2,1)S(1)} async-done(((bf16[256,4,200]{2,1,0:T(4,128)(2,1)}), bf16[256,4,200]{2,1,0:T(4,128)(2,1)S(1)}, u32[]{:S(2)}, u32[]{:S(2)}) %all-to-all-start) | async-done | bytes 409632 | tf_op jit(solution)/shard_map/all_to_all | solution.py:22
  53.5 128.7 %gather_fusion.1 = bf16[32768,200]{1,0:T(8,128)(2,1)} fusion(bf16[5120,200]{1,0:T(8,128)(2,1)S(1)} %pad_maximum_fusion.1, s32[32768]{0:T(1024)S(1)} %broadcast_clamp_fusion), kind=kCustom, calls=%fused_computation.1 | custom fusion | bytes 26345472 | tf_op jit(solution)/shard_map/gather | solution.py:24
  182.2 24.2 %fusion.2 = bf16[4096,200]{1,0:T(8,128)(2,1)S(1)} fusion(bf16[32768,200]{1,0:T(8,128)(2,1)} %gather_fusion.1, f32[4096,8]{1,0:T(8,128)} %copy.20), kind=kLoop, calls=%fused_computation.11 | loop fusion | flops 18841600 | bytes 14876672 | tf_op jit(solution)/shard_map/reduce_sum | solution.py:24
  207.7 3.2 maximum_convert_fusion
  211.0 6.7 gather_fusion.2
  219.5 8.8 all-to-all-start.1
  232.0 26.1 %all-to-all-done.1 = bf16[256,4,512]{2,1,0:T(4,128)(2,1)} async-done(((bf16[256,4,512]{2,1,0:T(4,128)(2,1)}), bf16[256,4,512]{2,1,0:T(4,128)(2,1)}, u32[]{:S(2)}, u32[]{:S(2)}) %all-to-all-start.1) | async-done | bytes 1048608 | tf_op jit(solution)/shard_map/all_to_all | solution.py:22
  259.4 4.9 pad_maximum_fusion
  264.3 135.2 %gather_fusion.3 = bf16[32768,512]{1,0:T(8,128)(2,1)} fusion(bf16[5120,512]{1,0:T(8,128)(2,1)} %pad_maximum_fusion, s32[32768]{0:T(1024)S(1)} %broadcast_clamp_fusion), kind=kCustom, calls=%fused_computation.3 | custom fusion | bytes 67239936 | tf_op jit(solution)/shard_map/gather | solution.py:24
  399.6 27.8 %fusion = bf16[4096,512]{1,0:T(8,128)(2,1)S(1)} fusion(bf16[32768,512]{1,0:T(8,128)(2,1)} %gather_fusion.3, f32[4096,8]{1,0:T(8,128)S(1)} %copy-done), kind=kLoop, calls=%fused_computation.7 | loop fusion | flops 48234496 | bytes 37879808 | tf_op jit(solution)/shard_map/reduce_sum | solution.py:24
  433.5 73.9 %all-reduce = (f32[]{:T(128)}, f32[]{:T(128)}) all-reduce(f32[]{:T(128)} %multiply_reduce_fusion, f32[]{:T(128)} %convert_reduce_fusion), channel_id=1, replica_groups=mesh['graph'=256] {'graph'}, use_global_device_ids=true, to_apply=%region_5.6 | all-reduce | flops 2 | bytes 16 | tf_op jit(solution)/shard_map/psum | solution.py:34
  507.9 4.6 fusion.20
  512.6 214.3 %scatter_custom_fusion = f32[5120,512]{1,0:T(8,128)} fusion(s32[32768]{0:T(1024)S(1)} %reshape.119, f32[4096,512]{1,0:T(8,128)} %fusion.20, f32[32768]{0:T(1024)S(1)} %mul.60, f32[]{:T(128)} %constant.6.clone.1), kind=kCustom, calls=%fused_computation.9 | custom fusion | flops 33554432 | bytes 19005444 | tf_op jit(solution)/shard_map/scatter-add | solution.py:39
  726.9 3.1 slice.17
  732.9 8.3 all-to-all-start.2
  741.8 7.9 slice.16
  751.2 42.0 %all-to-all-done.2 = f32[256,4,512]{2,1,0:T(4,128)} async-done(((f32[256,4,512]{2,1,0:T(4,128)}), f32[256,4,512]{2,1,0:T(4,128)}, u32[]{:S(2)}, u32[]{:S(2)}) %all-to-all-start.2) | async-done | bytes 2097184 | tf_op jit(solution)/shard_map/all_to_all | solution.py:40
  793.2 2.9 all_to_all.26
  796.1 14.7 %scatter_custom_fusion.1 = f32[4096,512]{1,0:T(8,128)} fusion(f32[4096,512]{1,0:T(8,128)} %slice.16, s32[1024]{0:T(1024)S(1)} %reshape.127, f32[1024,512]{1,0:T(8,128)} %all_to_all.26, f32[]{:T(128)} %constant.6.clone.1, pred[1024]{0:T(1024)(128)(4,1)S(1)} %lt.41), kind=kCustom, calls=%fused_computation.21 | custom fusion | flops 1048576 | bytes 10487296 | tf_op jit(solution)/shard_map/scatter-add | solution.py:41
  810.8 6.5 fusion.6
  818.5 248.3 %all-reduce.4.cloned.1.call-done = (f32[200,512]{1,0:T(8,128)}, f32[512,107]{0,1:T(8,128)}) async-done(((f32[200,512]{1,0:T(8,128)}, f32[512,107]{0,1:T(8,128)}), (f32[200,512]{1,0:T(8,128)}, f32[512,107]{0,1:T(8,128)})) %all-reduce.4.cloned.1.call-update) | async-done | bytes 628752 | tf_op jit(solution)/shard_map/psum | solution.py:43
  (67 shorter events, 32.1 us)
Async XLA Ops:
  8.0 0.7 copy-start.6
  11.8 4.2 copy-start.1
  11.8 4.2 copy-start.15
  15.8 16.2 %copy-start.9 = (s32[4096,8]{0,1:T(8,128)S(1)}, s32[4096,8]{0,1:T(8,128)}, u32[]{:S(2)}) copy-start(s32[4096,8]{0,1:T(8,128)} %param.14) | copy-start | bytes 393220
  17.3 33.9 %all-to-all-start = ((bf16[256,4,200]{2,1,0:T(4,128)(2,1)}), bf16[256,4,200]{2,1,0:T(4,128)(2,1)S(1)}, u32[]{:S(2)}, u32[]{:S(2)}) async-start(bf16[256,4,200]{2,1,0:T(4,128)(2,1)} %broadcast_select_fusion.1), calls=%async_computation | async-start | bytes 1048576 | tf_op jit(solution)/shard_map/all_to_all | solution.py:22
  32.0 1.7 copy-start.14
  182.2 25.5 %copy-start.11 = (f32[200,512]{1,0:T(8,128)S(1)}, f32[200,512]{1,0:T(8,128)}, u32[]{:S(2)}) copy-start(f32[200,512]{1,0:T(8,128)} %param.10) | copy-start | bytes 1228804
  206.4 1.3 copy-start.2
  218.0 10.4 copy-start
  219.5 9.9 copy-start.10
  219.5 38.6 %all-to-all-start.1 = ((bf16[256,4,512]{2,1,0:T(4,128)(2,1)}), bf16[256,4,512]{2,1,0:T(4,128)(2,1)}, u32[]{:S(2)}, u32[]{:S(2)}) async-start(bf16[256,4,512]{2,1,0:T(4,128)(2,1)} %broadcast_select_fusion), calls=%async_computation.1 | async-start | bytes 2097152 | tf_op jit(solution)/shard_map/all_to_all | solution.py:22
  228.3 3.0 copy-start.13
  399.5 27.8 %copy-start.8 = (f32[512,107]{0,1:T(8,128)S(1)}, f32[512,107]{0,1:T(8,128)}, u32[]{:S(2)}) copy-start(f32[512,107]{0,1:T(8,128)} %param.11) | copy-start | bytes 657412
  427.3 2.0 copy-start.4
  427.3 2.3 copy-start.12
  732.9 8.7 copy-start.7
  732.9 60.2 %all-to-all-start.2 = ((f32[256,4,512]{2,1,0:T(4,128)}), f32[256,4,512]{2,1,0:T(4,128)}, u32[]{:S(2)}, u32[]{:S(2)}) async-start(f32[256,4,512]{2,1,0:T(4,128)} %all_to_all.24), calls=%async_computation.2 | async-start | bytes 4194304 | tf_op jit(solution)/shard_map/all_to_all | solution.py:40
  741.2 325.6 %all-reduce.4.cloned.1.call-start = ((), (), s32[]{:S(2)}) async-start(), calls=%async_computation.3 | async-start | bytes 1277952 | tf_op jit(solution)/shard_map/psum | solution.py:43
  741.8 7.9 copy-start.5
  796.1 14.7 %copy-start.3 = (bf16[4096,200]{1,0:T(8,128)(2,1)S(1)}, bf16[4096,200]{1,0:T(8,128)(2,1)}, u32[]{:S(2)}) copy-start(bf16[4096,200]{1,0:T(8,128)(2,1)} %copy-done.2) | copy-start | bytes 4915204
Sparse Core Ops, SparseCore 0:
  817.4 249.3 all-reduce.3
where the time goes:
time: 1090 us; the launch traced here: 1080 us
  waiting for transfers between devices  332 us (30%)
  local copies, waits for them, and re-layouts  313 us (29%)
  other arithmetic  293 us (27%)
  blocking collectives  73.9 us (7%)
  starting transfers between devices  32 us (3%)
  matrix products  17.3 us (2%)
  between operations  16.9 us (2%)
    gather x2, local copies, waits for them, and re-layouts, aggregate(): ext_rows[edge_src].astype(jnp.float32) * edge_wt[:, :, None]  264 us
    psum x1, waiting for transfers between devices, device_step(): lax.psum(jnp.einsum('nf,nh->fh', z_one, d_y1, preferred_element_type=jnp....  248 us
    scatter-add x1, other arithmetic, device_step(): jax.ops.segment_sum(contrib, flat_src, num_segments=row_count + dev_count...  214 us
    psum x1, blocking collectives, device_step(): lax.psum(jnp.sum(mask_f[:, None] * onehot * log_prob), 'graph')  73.9 us
    reduce_sum x2, other arithmetic, aggregate(): jnp.sum(ext_rows[edge_src].astype(jnp.float32) * edge_wt[:, :, None], axi...  51.9 us
    all_to_all x1, waiting for transfers between devices, device_step(): returned = lax.all_to_all(ext_grad[row_count:], 'graph', 0, 0, tiled=True)  42 us
    all_to_all x2, waiting for transfers between devices, aggregate(): incoming = lax.all_to_all(outgoing, 'graph', 0, 0, tiled=True)  41.6 us
    all_to_all x2, starting transfers between devices, aggregate(): incoming = lax.all_to_all(outgoing, 'graph', 0, 0, tiled=True)  23.5 us
  transfers between devices with their start and end apart: 4, of which 4 were waited for; matrix products, arithmetic and copies ran while one was open for 2% of the time, Pallas kernels for 0%

commit v1 on v0

v1 whole, which is shorter than its diff:
```python
import functools

import jax
import jax.numpy as jnp
from jax import lax
from jax.experimental import pallas as pl
from jax.experimental.pallas import tpu as pltpu
from jax.sharding import PartitionSpec as P


F32, BF16, I32 = jnp.float32, jnp.bfloat16, jnp.int32
LANES = 128
CHUNK_ROWS = 128
HIDDEN_ROWS = 256
CHUNKS = 4
VMEM_CAP = 60 * 2**20
MESH = pl.DeviceIdType.MESH


def params(**kw):
    return pltpu.CompilerParams(vmem_limit_bytes=VMEM_CAP, **kw)


def spread_rows(dst, rows_ref, base, width):
    parts = width // LANES
    count = rows_ref.shape[0]

    block = 128

    def body(i, _):
        r = pl.multiple_of(i * block, block)
        vals = rows_ref[pl.ds(r, block), :].astype(F32)
        for c in range(parts):
            dst[pl.ds((base + r) * parts + c, block, stride=parts), :] = vals[:, c * LANES:(c + 1) * LANES]
        return 0

    lax.fori_loop(0, count // block, body, 0)


def spread_lists(dst, lists_ref, base, parts):
    count, size = lists_ref.shape[:2]
    group = 16

    def body(i, _):
        for u in range(group):
            q = i * group + u
            vals = lists_ref[q].astype(F32)
            for c in range(parts):
                dst[pl.ds((base + q * size) * parts + c, size, stride=parts), :] = vals[:, c * LANES:(c + 1) * LANES]
        return 0

    lax.fori_loop(0, count // group, body, 0)


def join_parts(src, rows, parts):
    return jnp.concatenate([src[pl.ds(c, rows, stride=parts), :].astype(BF16) for c in range(parts)], axis=1)


def pick_kernel(idx, rows_ref, out, ext, stage):
    count = rows_ref.shape[0]
    lists, size = out.shape[:2]
    picks = lists * size
    gap = picks + 8
    group = 128 // size
    ext[pl.ds(2 * count, 8), :] = jnp.zeros((8, LANES), F32)
    spread_rows(ext, rows_ref, 0, 2 * LANES)

    def body(i, _):
        lo = idx.at[pl.ds(pl.multiple_of(i * 128, 128), 128)]
        for u in range(128):
            stage[pl.ds(i * 128 + u, 2, stride=gap), :] = ext[pl.ds(pl.multiple_of(lo[u], 2), 2), :]
        for u in range(group):
            for c in range(2):
                vals = stage[pl.ds(c * gap + i * 128 + u * size, size), :]
                out[i * group + u, :, c * LANES:(c + 1) * LANES] = vals.astype(BF16)
        return 0

    lax.fori_loop(0, picks // 128, body, 0)


def pick_rows(idx, rows, size):
    picks, count = idx.shape[0], rows.shape[0]
    return pl.pallas_call(
        pick_kernel,
        in_specs=[pl.BlockSpec(memory_space=pltpu.SMEM), pl.BlockSpec(memory_space=pltpu.VMEM)],
        out_specs=pl.BlockSpec(memory_space=pltpu.VMEM),
        out_shape=jax.ShapeDtypeStruct((picks // size, size, 2 * LANES), BF16),
        scratch_shapes=[pltpu.VMEM((2 * count + 8, LANES), F32), pltpu.VMEM((2 * (picks + 8), LANES), F32)],
        compiler_params=params(),
        name="pick_rows",
    )(idx, rows)


def index_copies(step, src, bufs, sems):
    size = bufs[0].shape[0]
    return [
        pltpu.make_async_copy(src.at[pl.ds(pl.multiple_of((step * CHUNKS + b) * size, size), size)], bufs[b], sems.at[b])
        for b in range(CHUNKS)
    ]


def with_indices(src, bufs, sems, visit):
    step, last = pl.program_id(0), pl.num_programs(0) - 1
    now, later = index_copies(step, src, bufs, sems), index_copies(step + 1, src, bufs, sems)

    @pl.when(step == 0)
    def _():
        for copy in now:
            copy.start()

    for b in range(CHUNKS):
        now[b].wait()
        visit(b, bufs[b])

        @pl.when(step < last)
        def _():
            later[b].start()


def weighted_rows(ext, wts, acc, parts, deg, b, idx):
    for n in range(CHUNK_ROWS):
        total = None
        for k in range(deg):
            row = ext[pl.ds(pl.multiple_of(idx[n * deg + k], parts), parts), :]
            term = row * wts[pl.ds((b * CHUNK_ROWS + n) * deg + k, 1), :]
            total = term if total is None else total + term
        acc[pl.ds((b * CHUNK_ROWS + n) * parts, parts), :] = total


def layer_one_kernel(deg, src, wts, own, halo, z_out, ext, acc, sems, *bufs):
    @pl.when(pl.program_id(0) == 0)
    def _():
        spread_rows(ext, own, 0, 2 * LANES)
        spread_lists(ext, halo, own.shape[0], 2)

    with_indices(src, bufs, sems, functools.partial(weighted_rows, ext, wts, acc, 2, deg))
    z_out[...] = join_parts(acc, z_out.shape[0], 2)


def index_scratch(deg):
    return [pltpu.SemaphoreType.DMA((CHUNKS,))] + [pltpu.SMEM((CHUNK_ROWS * deg,), I32)] * CHUNKS


def layer_one(src, wts, own, halo, deg):
    rows, halo_rows = own.shape[0], halo.shape[0] * halo.shape[1]
    step_rows = CHUNK_ROWS * CHUNKS
    return pl.pallas_call(
        functools.partial(layer_one_kernel, deg),
        grid=(rows // step_rows,),
        in_specs=[
            pl.BlockSpec(memory_space=pl.ANY),
            pl.BlockSpec((step_rows * deg, LANES), lambda i: (i, 0)),
            pl.BlockSpec((rows, 2 * LANES), lambda i: (0, 0)),
            pl.BlockSpec(halo.shape, lambda i: (0, 0, 0)),
        ],
        out_specs=pl.BlockSpec((step_rows, 2 * LANES), lambda i: (i, 0)),
        out_shape=jax.ShapeDtypeStruct((rows, 2 * LANES), BF16),
        scratch_shapes=[
            pltpu.VMEM(((rows + halo_rows) * 2, LANES), F32),
            pltpu.VMEM((step_rows * 2, LANES), F32),
        ] + index_scratch(deg),
        compiler_params=params(),
        name="layer_one",
    )(src, wts, own, halo)


def hidden_rows(z, w):
    return jnp.maximum(jnp.dot(z, w, preferred_element_type=F32), 0.0).astype(BF16)


def spread_hidden(ext, load, count, w_ref, base):
    parts = w_ref.shape[1] // LANES
    block = HIDDEN_ROWS

    def body(i, _):
        r = pl.multiple_of(i * block, block)
        h = hidden_rows(load(r, block), w_ref[...]).astype(F32)
        for c in range(parts):
            ext[pl.ds((base + r) * parts + c, block, stride=parts), :] = h[:, c * LANES:(c + 1) * LANES]
        return 0

    lax.fori_loop(0, count // block, body, 0)


def layer_two_kernel(deg, classes, src, wts, own, halo, w1, w2, lab, cnt, g_out, gw_out, loss_out, ext, acc, sems, *bufs):
    parts = w1.shape[1] // LANES
    step = pl.program_id(0)

    @pl.when(step == 0)
    def _():
        count = own.shape[0]
        spread_hidden(ext, lambda r, n: own[pl.ds(r, n), :], count, w1, 0)
        spread_lists(acc, halo, 0, 2)
        pair = lambda r, n: [acc[pl.ds(2 * r + c, n, stride=2), :].astype(BF16) for c in range(2)]
        spread_hidden(ext, lambda r, n: jnp.concatenate(pair(r, n), axis=1), halo.shape[0] * halo.shape[1], w1, count)
        gw_out[...] = jnp.zeros_like(gw_out)
        loss_out[...] = jnp.zeros_like(loss_out)

    with_indices(src, bufs, sems, functools.partial(weighted_rows, ext, wts, acc, parts, deg))

    rows = g_out.shape[0]
    z = join_parts(acc, rows, parts)
    logits = jnp.dot(z, w2[...], preferred_element_type=F32)
    col = lax.broadcasted_iota(I32, logits.shape, 1)
    real = col < classes
    peak = jnp.max(jnp.where(real, logits, -jnp.inf), axis=1, keepdims=True)
    shifted = logits - peak
    norm = jnp.log(jnp.sum(jnp.where(real, jnp.exp(shifted), 0.0), axis=1, keepdims=True))
    log_prob = shifted - norm
    label = lab[...]
    hit = col == label
    mask = (label >= 0).astype(F32)
    loss_out[...] += jnp.sum(jnp.where(hit, log_prob, 0.0).reshape(rows // 8, 8, LANES), axis=0)
    prob = jnp.where(real, jnp.exp(log_prob), 0.0)
    grad = ((prob - hit.astype(F32)) * (mask / cnt[0:1, :])).astype(BF16)
    g_out[...] = grad.astype(F32)
    gw_out[...] += lax.dot_general(z, grad, (((0,), (0,)), ((), ())), preferred_element_type=F32)


def layer_two(src, wts, own, halo, w1, w2, lab, cnt, deg, classes):
    rows, halo_rows, hid = own.shape[0], halo.shape[0] * halo.shape[1], w1.shape[1]
    step_rows = CHUNK_ROWS * CHUNKS
    parts = hid // LANES
    whole = lambda a: pl.BlockSpec(a.shape, lambda i: (0, 0))
    return pl.pallas_call(
        functools.partial(layer_two_kernel, deg, classes),
        grid=(rows // step_rows,),
        in_specs=[
            pl.BlockSpec(memory_space=pl.ANY),
            pl.BlockSpec((step_rows * deg, LANES), lambda i: (i, 0)),
            whole(own), pl.BlockSpec(halo.shape, lambda i: (0, 0, 0)), whole(w1), whole(w2),
            pl.BlockSpec((step_rows, 1), lambda i: (i, 0)),
            whole(cnt),
        ],
        out_specs=[
            pl.BlockSpec((step_rows, LANES), lambda i: (i, 0)),
            pl.BlockSpec((hid, LANES), lambda i: (0, 0)),
            pl.BlockSpec((8, LANES), lambda i: (0, 0)),
        ],
        out_shape=[
            jax.ShapeDtypeStruct((rows, LANES), F32),
            jax.ShapeDtypeStruct((hid, LANES), F32),
            jax.ShapeDtypeStruct((8, LANES), F32),
        ],
        scratch_shapes=[
            pltpu.VMEM(((rows + halo_rows) * parts, LANES), F32),
            pltpu.VMEM((step_rows * parts, LANES), F32),
        ] + index_scratch(deg),
        compiler_params=params(),
        name="layer_two",
    )(src, wts, own, halo, w1, w2, lab, cnt)


def fill_zero(refs, rows):
    def body(i, _):
        for ref in refs:
            ref[pl.ds(pl.multiple_of(i * 64, 64), 64), :] = jnp.zeros((64, LANES), F32)
        return 0

    lax.fori_loop(0, rows // 64, body, 0)


def tree_sum(vals):
    while len(vals) > 1:
        vals = [vals[i] + vals[i + 1] for i in range(0, len(vals) - 1, 2)] + ([vals[-1]] if len(vals) % 2 else [])
    return vals[0]


def scatter_kernel(deg, src, wts, grad, out, halo_out, sems, *rest):
    bufs, accs = rest[:CHUNKS], rest[CHUNKS:]
    step = pl.program_id(0)

    @pl.when(step == 0)
    def _():
        fill_zero(accs, accs[0].shape[0])

    def visit(b, idx):
        for n in range(CHUNK_ROWS):
            row = grad[pl.ds(b * CHUNK_ROWS + n, 1), :]
            todo = []
            for k in range(deg):
                at = idx[n * deg + k]
                term = row * wts[pl.ds((b * CHUNK_ROWS + n) * deg + k, 1), :]
                todo.append((accs[k], at, accs[k][pl.ds(at, 1), :] + term))
            for ref, at, val in todo:
                ref[pl.ds(at, 1), :] = val

    with_indices(src, bufs, sems, visit)

    @pl.when(step == pl.num_programs(0) - 1)
    def _():
        def body(i, _):
            s = pl.ds(pl.multiple_of(i * 64, 64), 64)
            out[s, :] = tree_sum([a[s, :] for a in accs])
            return 0

        rows = out.shape[0]
        lax.fori_loop(0, rows // 64, body, 0)
        count, size = halo_out.shape[:2]

        def lists(i, _):
            for u in range(16):
                s = pl.ds(pl.multiple_of(rows + (i * 16 + u) * size, size), size)
                halo_out[i * 16 + u] = tree_sum([a[s, :] for a in accs])
            return 0

        lax.fori_loop(0, count // 16, lists, 0)


def scatter_back(src, wts, grad, count, size, deg):
    rows = grad.shape[0]
    ext_rows = rows + count * size
    step_rows = CHUNK_ROWS * CHUNKS
    return pl.pallas_call(
        functools.partial(scatter_kernel, deg),
        grid=(rows // step_rows,),
        in_specs=[
            pl.BlockSpec(memory_space=pl.ANY),
            pl.BlockSpec((step_rows * deg, LANES), lambda i: (i, 0)),
            pl.BlockSpec((step_rows, LANES), lambda i: (i, 0)),
        ],
        out_specs=[
            pl.BlockSpec((rows, LANES), lambda i: (0, 0)),
            pl.BlockSpec((count, size, LANES), lambda i: (0, 0, 0)),
        ],
        out_shape=[
            jax.ShapeDtypeStruct((rows, LANES), F32),
            jax.ShapeDtypeStruct((count, size, LANES), F32),
        ],
        scratch_shapes=index_scratch(deg) + [pltpu.VMEM((ext_rows, LANES), F32)] * deg,
        compiler_params=params(),
        name="scatter_back",
    )(src, wts, grad)


def first_grad_kernel(lists, idx, agg, back, z_ref, w1, w2t, out, *accs):
    rows = agg.shape[0]
    spare = accs[0].shape[0] - rows
    fill_zero(accs, rows)
    for a in accs:
        a[pl.ds(rows, spare), :] = jnp.zeros((spare, LANES), F32)

    def fold(i, _):
        lo = idx.at[pl.ds(pl.multiple_of(i * 128, 128), 128)]
        for u in range(0, 128, lists):
            got = back.at[i * (128 // lists) + u // lists]
            todo = [(accs[j], lo[u + j], accs[j][pl.ds(lo[u + j], 1), :] + got[pl.ds(j, 1), :]) for j in range(lists)]
            for ref, at, val in todo:
                ref[pl.ds(at, 1), :] = val
        return 0

    lax.fori_loop(0, idx.shape[0] // 128, fold, 0)
    out[...] = jnp.zeros_like(out)
    block = 512

    def body(i, _):
        s = pl.ds(pl.multiple_of(i * block, block), block)
        p = agg[s, :] + tree_sum([a[s, :] for a in accs])
        hi = p.astype(BF16)
        rest = p - hi.astype(F32)
        mid = rest.astype(BF16)
        low = (rest - mid.astype(F32)).astype(BF16)
        dh = jnp.dot(jnp.concatenate([low, mid, hi], axis=1), w2t[...], preferred_element_type=F32)
        z = z_ref[s, :]
        h = hidden_rows(z, w1[...]).astype(F32)
        g = jnp.where(h > 0, dh, 0.0).astype(BF16)
        out[...] += lax.dot_general(z, g, (((0,), (0,)), ((), ())), preferred_element_type=F32)
        return 0

    lax.fori_loop(0, rows // block, body, 0)


def first_grad(idx, agg, back, z, w1, w2t, lists):
    rows = z.shape[0]
    vm = pl.BlockSpec(memory_space=pltpu.VMEM)
    return pl.pallas_call(
        functools.partial(first_grad_kernel, lists),
        grid=(1,),
        in_specs=[
            pl.BlockSpec(memory_space=pltpu.SMEM),
            pl.BlockSpec((rows, LANES), lambda i: (0, 0)),
            vm, vm, vm, vm,
        ],
        out_specs=vm,
        out_shape=jax.ShapeDtypeStruct((z.shape[1], w1.shape[1]), F32),
        scratch_shapes=[pltpu.VMEM((rows + 8, LANES), F32)] * lists,
        compiler_params=params(),
        name="first_grad",
    )(idx, agg, back, z, w1, w2t)


def place():
    me = lax.axis_index("graph")
    return lax.rem(me, 2), lax.rem(me // 2, 4), lax.rem(me // 8, 4), me // 32


def index_of(c, x, y, z):
    return ((z * 4 + y) * 4 + x) * 2 + c


def ring_peers(zs):
    c, x, y, z = place()
    return (
        [index_of(1 - c, x, y, z)],
        [index_of(c, lax.rem(x + d, 4), y, z) for d in range(1, 4)],
        [index_of(c, x, lax.rem(y + d, 4), z) for d in range(1, 4)],
        [index_of(c, x, y, lax.rem(z + d, zs)) for d in range(1, zs)],
    )


def greet(groups):
    barrier = pltpu.get_barrier_semaphore()
    peers = [p for g in groups for p in g]
    for p in peers:
        pl.semaphore_signal(barrier, inc=1, device_id=(p,), device_id_type=MESH)
    pl.semaphore_wait(barrier, len(peers))


def count_kernel(zs, val, out, mine, got, send, recv):
    groups = ring_peers(zs)
    greet(groups)
    mine[0] = val[...]
    slot = 0
    for s, peers in enumerate(groups):
        copies = []
        for p in peers:
            copies.append(pltpu.make_async_remote_copy(
                src_ref=mine.at[s], dst_ref=got.at[slot], send_sem=send.at[slot], recv_sem=recv.at[slot],
                device_id=(p,), device_id_type=MESH))
            slot += 1
        for copy in copies:
            copy.start()
        for copy in copies:
            copy.wait()
        mine[s + 1] = mine[s] + tree_sum([got[slot - len(peers) + i] for i in range(len(peers))])
    out[...] = mine[len(groups)]


def count_all(val, zs):
    n = 1 + 3 + 3 + zs - 1
    return pl.pallas_call(
        functools.partial(count_kernel, zs),
        in_specs=[pl.BlockSpec(memory_space=pltpu.VMEM)],
        out_specs=pl.BlockSpec(memory_space=pltpu.VMEM),
        out_shape=jax.ShapeDtypeStruct(val.shape, F32),
        scratch_shapes=[
            pltpu.VMEM((5,) + val.shape, F32), pltpu.VMEM((n,) + val.shape, F32),
            pltpu.SemaphoreType.DMA((n,)), pltpu.SemaphoreType.DMA((n,)),
        ],
        compiler_params=pltpu.CompilerParams(collective_id=1, has_side_effects=True),
        name="count_all",
    )(val)


def sum_kernel(zs, parts, g1, g2, loss, cnt, o_g1, o_g2, o_loss, val, s1, s2, s3, r1, r2, r3, r4, o0, o1, o2, send, recv):
    c, x, y, z = place()
    cores, xs, ys, zps = groups = ring_peers(zs)
    feat, hid = o_g1.shape[0], g2.shape[0]
    first = parts * feat
    for p in range(parts):
        val[pl.ds(p * feat, feat), :] = g1[pl.ds(0, feat), p * LANES:(p + 1) * LANES]
    val[pl.ds(first, hid), :] = g2[...]
    val[pl.ds(first + hid, 8), :] = loss[...]
    spare = val.shape[0] - first - hid - 8
    val[pl.ds(first + hid + 8, spare), :] = jnp.zeros((spare, LANES), F32)
    greet(groups)
    h, q, e = r1.shape[0], s2.shape[1], s3.shape[1]
    used = [0]

    def remote(src, dst, peer):
        i = used[0]
        used[0] += 1
        return pltpu.make_async_remote_copy(
            src_ref=src, dst_ref=dst, send_sem=send.at[i], recv_sem=recv.at[i], device_id=(peer,), device_id_type=MESH)

    def run(copies):
        for copy in copies:
            copy.start()
        for copy in copies:
            copy.wait()

    def at(i, size, base=0):
        return pl.ds(pl.multiple_of(base + i * size, 8), size)

    routes = ((x, xs, y, ys), (y, ys, x, xs))
    half = h // 2
    run([remote(val.at[at(1 - c, h)], r1, cores[0])])
    s1[...] = val[at(c, h), :] + r1[...]
    run([remote(s1.at[at(lax.rem(a + d, 4), q, k * half)], r2.at[k, d - 1], pa[d - 1])
         for d in range(1, 4) for k, (a, pa, _, _) in enumerate(routes)])
    for k, (a, _, _, _) in enumerate(routes):
        s2[k] = (s1[at(a, q, k * half), :] + r2[k, 0]) + (r2[k, 1] + r2[k, 2])
    run([remote(s2.at[k, at(lax.rem(b + d, 4), e)], r3.at[k, d - 1], pb[d - 1])
         for d in range(1, 4) for k, (_, _, b, pb) in enumerate(routes)])
    for k, (_, _, b, _) in enumerate(routes):
        s3[k] = (s2[k, at(b, e), :] + r3[k, 0]) + (r3[k, 1] + r3[k, 2])
    r4[z] = s3[...]
    run([remote(s3, r4.at[z], zps[d - 1]) for d in range(1, zs)])
    for k, (_, _, b, _) in enumerate(routes):
        o2[k, at(b, e), :] = tree_sum([r4[i, k] for i in range(zs)])
    run([remote(o2.at[k, at(b, e)], o2.at[k, at(b, e)], pb[d - 1])
         for d in range(1, 4) for k, (_, _, b, pb) in enumerate(routes)])
    for k, (a, _, _, _) in enumerate(routes):
        o1[at(a, q, k * half), :] = o2[k]
    run([remote(o2.at[k], o1.at[at(a, q, k * half)], pa[d - 1])
         for d in range(1, 4) for k, (a, pa, _, _) in enumerate(routes)])
    o0[at(c, h), :] = o1[...]
    run([remote(o1, o0.at[at(c, h)], cores[0])])
    for p in range(parts):
        o_g1[:, p * LANES:(p + 1) * LANES] = o0[pl.ds(p * feat, feat), :]
    o_g2[...] = o0[pl.ds(first, hid), :]
    total = jnp.sum(o0[pl.ds(first + hid, 8), :], axis=0, keepdims=True)
    o_loss[...] = jnp.broadcast_to(-jnp.sum(total, axis=1, keepdims=True) / cnt[0:1, :], o_loss.shape)


def sum_all(g1, g2, loss, cnt, feat, zs):
    hid = g1.shape[1]
    parts = hid // LANES
    used = parts * feat + g2.shape[0] + 8
    rows = used + -used % 512
    h, q, e = rows // 2, rows // 16, rows // 64
    n = 2 * (1 + 6 + 6) + zs - 1
    buf = lambda *s: pltpu.VMEM(s + (LANES,), F32)
    vm = pl.BlockSpec(memory_space=pltpu.VMEM)
    return pl.pallas_call(
        functools.partial(sum_kernel, zs, parts),
        in_specs=[vm] * 4,
        out_specs=[vm] * 3,
        out_shape=[
            jax.ShapeDtypeStruct((feat, hid), F32),
            jax.ShapeDtypeStruct(g2.shape, F32),
            jax.ShapeDtypeStruct((8, LANES), F32),
        ],
        scratch_shapes=[
            buf(rows), buf(h), buf(2, q), buf(2, e), buf(h), buf(2, 3, q), buf(2, 3, e), buf(zs, 2, e),
            buf(rows), buf(h), buf(2, q),
            pltpu.SemaphoreType.DMA((n,)), pltpu.SemaphoreType.DMA((n,)),
        ],
        compiler_params=pltpu.CompilerParams(collective_id=0, has_side_effects=True, vmem_limit_bytes=32 * 2**20),
        name="sum_all",
    )(g1, g2, loss, cnt)


def solution(mesh):
    devs = mesh.shape["graph"]
    zs = devs // 32

    def device_step(feats, w_one, w_two, send_idx, send_count, edge_src, edge_wt, labels, label_mask):
        rows, feat_in = feats.shape
        hid, classes = w_two.shape
        lists, deg = send_idx.shape[1], edge_src.shape[1]

        list_ok = jnp.arange(lists)[None, :] < send_count[:, None]
        list_rows = jnp.where(list_ok, send_idx, rows).reshape(devs * lists)
        src = edge_src.reshape(rows * deg)
        wts = jnp.broadcast_to(edge_wt[:, :, None], (rows, deg, LANES)).reshape(rows * deg, LANES)
        w1 = jnp.pad(w_one.astype(BF16), ((0, 2 * LANES - feat_in), (0, 0)))
        w2 = jnp.pad(w_two.astype(BF16), ((0, 0), (0, LANES - classes)))
        own = jnp.pad(feats, ((0, 0), (0, 2 * LANES - feat_in)))
        lab = jnp.where(label_mask == 1, labels, -1)[:, None]
        local_count = jnp.broadcast_to(jnp.sum(label_mask.astype(F32)), (8, LANES))

        def exchange(block):
            return lax.all_to_all(block, "graph", 0, 0, tiled=True)

        halo_one = exchange(pick_rows(list_rows * 2, own, lists))
        cnt = count_all(local_count, zs)
        z_one = layer_one(src * 2, wts, own, halo_one, deg)
        halo_two = exchange(pick_rows(list_rows * 2, z_one, lists))
        grad, gw_two, loss_part = layer_two(src * (hid // LANES), wts, z_one, halo_two, w1, w2, lab, cnt, deg, classes)
        agg, halo_grad = scatter_back(src, wts, grad, devs, lists, deg)
        back = exchange(halo_grad)
        gw_one = first_grad(list_rows, agg, back, z_one, w1, jnp.tile(w2.T, (3, 1)), lists)

        grad_one, grad_two, loss = sum_all(gw_one, gw_two, loss_part, cnt, feat_in, zs)
        return loss[0, 0], grad_one, grad_two[:, :classes]

    row_spec = P("graph", None)
    vec_spec = P("graph")

    return jax.shard_map(device_step, mesh=mesh, in_specs=(row_spec, P(), P(), row_spec, vec_spec, row_spec, row_spec, vec_spec, vec_spec), out_specs=(P(), P(), P()), check_vma=False)
```

time: 1090 us -> 268 us (0.25)
  waiting for transfers between devices: 332 us -> 34.2 us
  other arithmetic: 293 us -> 2.67 us
  local copies, waits for them, and re-layouts: 313 us -> 33 us
  Pallas kernels: 0 us -> 163 us
  blocking collectives: 73.9 us -> 0 us
  matrix products: 17.3 us -> 0 us
  between operations: 16.9 us -> 0.88 us
    gather x6 -> x0, local copies, waits for them, and re-layouts: 275 us -> none  [the longest x2 264 us: aggregate(): ext_rows[edge_src].astype(jnp.float32) * edge_wt[:, :, None]]
    psum x1 -> x0, waiting for transfers between devices: 248 us -> none  [device_step(): lax.psum(jnp.einsum('nf,nh->fh', z_one, d_y1, preferred_element_type=jnp....]
    scatter-add x2 -> x0, other arithmetic: 229 us -> none  [the longest x1 214 us: device_step(): jax.ops.segment_sum(contrib, flat_src, num_segments=row_count + dev_count...]
    pallas_call x0 -> x8, Pallas kernels: none -> 163 us  [the longest x1 37.3 us: layer_two(): pl.pallas_call(functools.partial(layer_two_kernel, deg, classes), grid=(r...]
    psum x1 -> x0, blocking collectives: 73.9 us -> none  [device_step(): lax.psum(jnp.sum(mask_f[:, None] * onehot * log_prob), 'graph')]
    reduce_sum x5 -> x1, other arithmetic: 54 us -> 0.6 us  [device_step(): local_count = jnp.broadcast_to(jnp.sum(label_mask.astype(F32)), (8, LANES))]
    all_to_all x3, waiting for transfers between devices: 83.6 us -> 34.2 us  [exchange(): return lax.all_to_all(block, 'graph', 0, 0, tiled=True)]
    broadcast_in_dim x1 -> x4, local copies, waits for them, and re-layouts: 1.04 us -> 19.1 us  [the longest x2 15.8 us: device_step(): jnp.broadcast_to(edge_wt[:, :, None], (rows, deg, LANES))]
  transfers between devices with their start and end apart: 4 -> 3, of which waited for: 4 -> 2; matrix products, arithmetic and copies ran while one was open for 2% -> 4% of each run, Pallas kernels for 0% -> 8%
where the time goes in v1:
time: 268 us; the launch traced here: 265 us
  Pallas kernels  163 us (61%)
  waiting for transfers between devices  34.2 us (13%)
  local copies, waits for them, and re-layouts  33 us (12%)
  starting transfers between devices  30.9 us (12%)
    pallas_call x1, Pallas kernels, layer_two(): pl.pallas_call(functools.partial(layer_two_kernel, deg, classes), grid=(r...  37.3 us
    all_to_all x3, waiting for transfers between devices, exchange(): return lax.all_to_all(block, 'graph', 0, 0, tiled=True)  34.2 us
    pallas_call x1, Pallas kernels, sum_all(): pl.pallas_call(functools.partial(sum_kernel, zs, parts), in_specs=[vm] *...  31.4 us
    all_to_all x3, starting transfers between devices, exchange(): return lax.all_to_all(block, 'graph', 0, 0, tiled=True)  30.9 us
    pallas_call x1, Pallas kernels, scatter_back(): pl.pallas_call(functools.partial(scatter_kernel, deg), grid=(rows // step...  30 us
    pallas_call x1, Pallas kernels, layer_one(): pl.pallas_call(functools.partial(layer_one_kernel, deg), grid=(rows // st...  24.2 us
    pallas_call x1, Pallas kernels, count_all(): pl.pallas_call(functools.partial(count_kernel, zs), in_specs=[pl.BlockSpe...  20.4 us
    broadcast_in_dim x2, local copies, waits for them, and re-layouts, device_step(): jnp.broadcast_to(edge_wt[:, :, None], (rows, deg, LANES))  15.8 us
  transfers between devices with their start and end apart: 3, of which 2 were waited for; matrix products, arithmetic and copies ran while one was open for 4% of the time, Pallas kernels for 8%

profile of v1, /device:TPU:2, one launch (start us, length us, event | category | flops | bytes accessed | tf_op | source)
XLA Modules:
  0.0 264.9 jit_solution(14133853594167594460)
XLA Ops:
  2.2 3.2 %copy.27 = bf16[4096,200]{1,0:T(8,128)(2,1)S(1)} copy(bf16[4096,200]{0,1:T(8,128)(2,1)} %param.9) | data formatting | bytes 3276800 | tf_op args[0]
  5.4 1.6 pad.12.rows_ref.own
  7.0 3.9 %pick_rows.2 = bf16[256,4,256]{2,1,0:T(4,128)(2,1)} custom-call(s32[1024]{0:T(1024)} %broadcast_multiply_fusion.2.idx, bf16[4096,256]{1,0:T(8,128)(2,1)} %pad.12.rows_ref.own), custom_call_target="tpu_custom_call" | custom-call | tf_op jit(solution)/shard_map/pick_rows/pallas_call | solution.py:83
  10.9 14.7 %all-to-all-start = ((bf16[256,4,256]{2,1,0:T(4,128)(2,1)}), bf16[256,4,256]{2,1,0:T(4,128)(2,1)S(1)}, u32[]{:S(2)}, u32[]{:S(2)}) async-start(bf16[256,4,256]{2,1,0:T(4,128)(2,1)} %pick_rows.2), calls=%async_computation | async-start | bytes 1048576 | tf_op jit(solution)/shard_map/all_to_all | solution.py:564
  26.2 1.0 broadcast_in_dim.25
  27.9 1.0 reshape.22.src
  29.6 15.2 %all-to-all-done.halo = bf16[256,4,256]{2,1,0:T(4,128)(2,1)S(1)} async-done(((bf16[256,4,256]{2,1,0:T(4,128)(2,1)}), bf16[256,4,256]{2,1,0:T(4,128)(2,1)S(1)}, u32[]{:S(2)}, u32[]{:S(2)}) %all-to-all-start) | async-done | bytes 524320 | tf_op jit(solution)/shard_map/all_to_all | solution.py:564
  44.8 14.8 %broadcast_in_dim.26.wts = f32[32768,128]{1,0:T(8,128)} broadcast(f32[32768]{0:T(1024)S(1)} %broadcast_in_dim.25), dimensions={0} | broadcast | bytes 16908288 | tf_op jit(solution)/shard_map/broadcast_in_dim | solution.py:556
  59.6 24.2 %layer_one.1.rows_ref.own.z_ref = bf16[4096,256]{1,0:T(8,128)(2,1)} custom-call(s32[32768]{0:T(1024)} %get-tuple-element.30.src, f32[32768,128]{1,0:T(8,128)} %broadcast_in_dim.26.wts, bf16[4096,256]{1,0:T(8,128)(2,1)} %pad.12.rows_ref.own, bf16[256,4,256]{2,1,0:T(4,128)(2,1)} %copy-done.6), custom_call_target="tpu_custom_call" | custom-call | tf_op jit(solution)/shard_map/layer_one/pallas_call | solution.py:147
  83.8 3.9 %pick_rows.3 = bf16[256,4,256]{2,1,0:T(4,128)(2,1)} custom-call(s32[1024]{0:T(1024)} %broadcast_multiply_fusion.2.idx, bf16[4096,256]{1,0:T(8,128)(2,1)} %layer_one.1.rows_ref.own.z_ref), custom_call_target="tpu_custom_call" | custom-call | tf_op jit(solution)/shard_map/pick_rows/pallas_call | solution.py:83
  87.7 6.9 %all-to-all-start.1 = ((bf16[256,4,256]{2,1,0:T(4,128)(2,1)}), bf16[256,4,256]{2,1,0:T(4,128)(2,1)S(1)}, u32[]{:S(2)}, u32[]{:S(2)}) async-start(bf16[256,4,256]{2,1,0:T(4,128)(2,1)} %pick_rows.3), calls=%async_computation.1 | async-start | bytes 1048576 | tf_op jit(solution)/shard_map/all_to_all | solution.py:564
  96.2 1.2 broadcast_in_dim.29.val
  97.4 20.4 %count_all.1.cnt = f32[8,128]{1,0:T(8,128)} custom-call(f32[8,128]{1,0:T(8,128)} %broadcast_in_dim.29.val), custom_call_target="tpu_custom_call" | custom-call | tf_op jit(solution)/shard_map/count_all/pallas_call | solution.py:441
  117.8 2.0 copy.29.lab
  120.5 0.8 copy-done.4
  121.3 37.3 %layer_two.1 = (f32[4096,128]{1,0:T(8,128)}, f32[512,128]{1,0:T(8,128)}, f32[8,128]{1,0:T(8,128)}) custom-call(s32[32768]{0:T(1024)} %get-tuple-element.31.src, f32[32768,128]{1,0:T(8,128)} %broadcast_in_dim.26.wts, bf16[4096,256]{1,0:T(8,128)(2,1)} %layer_one.1.rows_ref.own.z_ref, bf16[256,4,256]{2,1,0:T(4,128)(2,1)} %copy-done.4, ...), custom_call_target="tpu_custom_call" | custom-call | tf_op jit(solution)/shard_map/layer_two/pallas_call | solution.py:225
  158.6 30.0 %scatter_back.1 = (f32[4096,128]{1,0:T(8,128)}, f32[256,4,128]{2,1,0:T(4,128)}) custom-call(s32[32768]{0:T(1024)} %copy-done.7, f32[32768,128]{1,0:T(8,128)} %broadcast_in_dim.26.wts, f32[4096,128]{1,0:T(8,128)} %get-tuple-element.11.grad), custom_call_target="tpu_custom_call" | custom-call | tf_op jit(solution)/shard_map/scatter_back/pallas_call | solution.py:314
  188.6 9.3 %all-to-all-start.2 = ((f32[256,4,128]{2,1,0:T(4,128)}), f32[256,4,128]{2,1,0:T(4,128)S(1)}, u32[]{:S(2)}, u32[]{:S(2)}) async-start(f32[256,4,128]{2,1,0:T(4,128)} %get-tuple-element.13), calls=%async_computation.2 | async-start | bytes 1048576 | tf_op jit(solution)/shard_map/all_to_all | solution.py:564
  198.1 19.1 %all-to-all-done.2.back = f32[256,4,128]{2,1,0:T(4,128)S(1)} async-done(((f32[256,4,128]{2,1,0:T(4,128)}), f32[256,4,128]{2,1,0:T(4,128)S(1)}, u32[]{:S(2)}, u32[]{:S(2)}) %all-to-all-start.2) | async-done | bytes 524320 | tf_op jit(solution)/shard_map/all_to_all | solution.py:564
  217.1 0.8 tile.4
  218.1 12.3 %first_grad.1.g1 = f32[256,512]{1,0:T(8,128)} custom-call(s32[1024]{0:T(1024)} %copy-done.13, f32[4096,128]{1,0:T(8,128)} %get-tuple-element.12.agg, f32[256,4,128]{2,1,0:T(4,128)} %copy-done.5, bf16[4096,256]{1,0:T(8,128)(2,1)} %layer_one.1.rows_ref.own.z_ref, bf16[256,512]{1,0:T(8,128)(2,1)} %pad.13.w1, bf16[384,512]{1,0:T(8,128)(2,1)} %bitcast.7), custom_call_target="tpu_custom_call" | custom-call | tf_op jit(solution)/shard_map/first_grad/pallas_call | solution.py:376
  230.4 1.0 copy-done
  231.4 31.4 %sum_all.1 = (f32[200,512]{1,0:T(8,128)S(1)}, f32[512,128]{1,0:T(8,128)S(1)}, f32[8,128]{1,0:T(8,128)S(1)}) custom-call(f32[256,512]{1,0:T(8,128)S(1)} %copy-done, f32[512,128]{1,0:T(8,128)S(1)} %copy-done.1, f32[8,128]{1,0:T(8,128)S(1)} %copy-done.3, f32[8,128]{1,0:T(8,128)S(1)} %copy-done.2), custom_call_target="tpu_custom_call" | custom-call | tf_op jit(solution)/shard_map/sum_all/pallas_call | solution.py:525
  262.8 0.8 copy.31
  (46 shorter events, 7.2 us)
Async XLA Ops:
  1.6 5.4 %copy-start.13 = (s32[1024]{0:T(1024)}, s32[1024]{0:T(1024)S(1)}, u32[]{:S(2)}) copy-start(s32[1024]{0:T(1024)S(1)} %reshape.21.idx) | copy-start | bytes 12292
  7.0 18.6 %copy-start.10 = (f32[4096,8]{0,1:T(8,128)S(1)}, f32[4096,8]{0,1:T(8,128)}, u32[]{:S(2)}) copy-start(f32[4096,8]{0,1:T(8,128)} %param.15) | copy-start | bytes 393220
  10.9 33.9 %all-to-all-start = ((bf16[256,4,256]{2,1,0:T(4,128)(2,1)}), bf16[256,4,256]{2,1,0:T(4,128)(2,1)S(1)}, u32[]{:S(2)}, u32[]{:S(2)}) async-start(bf16[256,4,256]{2,1,0:T(4,128)(2,1)} %pick_rows.2), calls=%async_computation | async-start | bytes 1048576 | tf_op jit(solution)/shard_map/all_to_all | solution.py:564
  25.6 1.7 copy-start.11
  28.9 30.7 %copy-start.7 = (s32[32768]{0:T(1024)}, s32[32768]{0:T(1024)S(1)}, u32[]{:S(2)}) copy-start(s32[32768]{0:T(1024)S(1)} %reshape.22.src) | copy-start | bytes 393220
  44.8 14.8 %copy-start.6 = (bf16[256,4,256]{2,1,0:T(4,128)(2,1)}, bf16[256,4,256]{2,1,0:T(4,128)(2,1)S(1)}, u32[]{:S(2)}) copy-start(bf16[256,4,256]{2,1,0:T(4,128)(2,1)S(1)} %all-to-all-done.halo) | copy-start | bytes 1572868
  83.8 10.9 %copy-start.9 = (f32[512,107]{0,1:T(8,128)S(1)}, f32[512,107]{0,1:T(8,128)}, u32[]{:S(2)}) copy-start(f32[512,107]{0,1:T(8,128)} %param.11) | copy-start | bytes 657412
  83.8 11.0 %copy-start.8 = (f32[200,512]{1,0:T(8,128)S(1)}, f32[200,512]{1,0:T(8,128)}, u32[]{:S(2)}) copy-start(f32[200,512]{1,0:T(8,128)} %param.10) | copy-start | bytes 1228804
  83.8 11.8 %copy-start.12 = (s32[4096]{0:T(1024)S(1)}, s32[4096]{0:T(1024)}, u32[]{:S(2)}) copy-start(s32[4096]{0:T(1024)} %param.17) | copy-start | bytes 49156
  83.8 34.0 %copy-start.14 = (s32[4096]{0:T(1024)S(1)}, s32[4096]{0:T(1024)}, u32[]{:S(2)}) copy-start(s32[4096]{0:T(1024)} %param.16) | copy-start | bytes 49156
  87.7 32.8 %all-to-all-start.1 = ((bf16[256,4,256]{2,1,0:T(4,128)(2,1)}), bf16[256,4,256]{2,1,0:T(4,128)(2,1)S(1)}, u32[]{:S(2)}, u32[]{:S(2)}) async-start(bf16[256,4,256]{2,1,0:T(4,128)(2,1)} %pick_rows.3), calls=%async_computation.1 | async-start | bytes 1048576 | tf_op jit(solution)/shard_map/all_to_all | solution.py:564
  120.5 0.8 copy-start.4
  188.6 28.5 %all-to-all-start.2 = ((f32[256,4,128]{2,1,0:T(4,128)}), f32[256,4,128]{2,1,0:T(4,128)S(1)}, u32[]{:S(2)}, u32[]{:S(2)}) async-start(f32[256,4,128]{2,1,0:T(4,128)} %get-tuple-element.13), calls=%async_computation.2 | async-start | bytes 1048576 | tf_op jit(solution)/shard_map/all_to_all | solution.py:564
  217.1 0.9 copy-start.5
  218.1 12.3 %copy-start.1 = (f32[512,128]{1,0:T(8,128)S(1)}, f32[512,128]{1,0:T(8,128)}, u32[]{:S(2)}) copy-start(f32[512,128]{1,0:T(8,128)} %get-tuple-element.14.g2) | copy-start | bytes 786436
  218.1 12.3 %copy-start.2 = (f32[8,128]{1,0:T(8,128)S(1)}, f32[8,128]{1,0:T(8,128)}, u32[]{:S(2)}) copy-start(f32[8,128]{1,0:T(8,128)} %count_all.1.cnt) | copy-start | bytes 12292
  218.1 12.3 %copy-start.3 = (f32[8,128]{1,0:T(8,128)S(1)}, f32[8,128]{1,0:T(8,128)}, u32[]{:S(2)}) copy-start(f32[8,128]{1,0:T(8,128)} %get-tuple-element.15.loss) | copy-start | bytes 12292
  230.4 1.0 copy-start

commit v2 on v1

--- a/solution.py
+++ b/solution.py
@@ -11,7 +11,7 @@
 F32, BF16, I32 = jnp.float32, jnp.bfloat16, jnp.int32
 LANES = 128
 CHUNK_ROWS = 128
-HIDDEN_ROWS = 256
+HIDDEN_ROWS = 512
 CHUNKS = 4
 VMEM_CAP = 60 * 2**20
 MESH = pl.DeviceIdType.MESH
@@ -125,6 +125,27 @@
             term = row * wts[pl.ds((b * CHUNK_ROWS + n) * deg + k, 1), :]
             total = term if total is None else total + term
         acc[pl.ds((b * CHUNK_ROWS + n) * parts, parts), :] = total
+
+
+def spread_kernel(wt, out):
+    deg = wt.shape[0]
+    for n in range(wt.shape[1]):
+        out[pl.ds(n * deg, deg), :] = jnp.broadcast_to(wt[:, n:n + 1], (deg, LANES))
+
+
+def spread_weights(wt):
+    deg, rows = wt.shape
+    block = 512
+    return pl.pallas_call(
+        spread_kernel,
+        grid=(rows // block,),
+        in_specs=[pl.BlockSpec((deg, block), lambda i: (0, i))],
+        out_specs=pl.BlockSpec((block * deg, LANES), lambda i: (i, 0)),
+        out_shape=jax.ShapeDtypeStruct((rows * deg, LANES), F32),
+        cost_estimate=pl.CostEstimate(flops=0, bytes_accessed=rows * deg * LANES * 4, transcendentals=0),
+        compiler_params=params(),
+        name="spread_weights",
+    )(wt)
 
 
 def layer_one_kernel(deg, src, wts, own, halo, z_out, ext, acc, sems, *bufs):
@@ -214,7 +235,7 @@
     prob = jnp.where(real, jnp.exp(log_prob), 0.0)
     grad = ((prob - hit.astype(F32)) * (mask / cnt[0:1, :])).astype(BF16)
     g_out[...] = grad.astype(F32)
-    gw_out[...] += lax.dot_general(z, grad, (((0,), (0,)), ((), ())), preferred_element_type=F32)
+    gw_out[...] += lax.dot_general(grad, z, (((0,), (0,)), ((), ())), preferred_element_type=F32)
 
 
 def layer_two(src, wts, own, halo, w1, w2, lab, cnt, deg, classes):
@@ -234,12 +255,12 @@
         ],
         out_specs=[
             pl.BlockSpec((step_rows, LANES), lambda i: (i, 0)),
-            pl.BlockSpec((hid, LANES), lambda i: (0, 0)),
+            pl.BlockSpec((LANES, hid), lambda i: (0, 0)),
             pl.BlockSpec((8, LANES), lambda i: (0, 0)),
         ],
         out_shape=[
             jax.ShapeDtypeStruct((rows, LANES), F32),
-            jax.ShapeDtypeStruct((hid, LANES), F32),
+            jax.ShapeDtypeStruct((LANES, hid), F32),
             jax.ShapeDtypeStruct((8, LANES), F32),
         ],
         scratch_shapes=[
@@ -417,7 +438,10 @@
 
 
 def count_kernel(zs, val, out, mine, got, send, recv):
-    groups = ring_peers(zs)
+    c, x, y, z = place()
+    plane = [index_of(lax.rem(c + i, 2), lax.rem(x + d, 4), y, z) for d in range(4) for i in range(2) if i or d]
+    _, _, ys, zps = ring_peers(zs)
+    groups = (plane, ys, zps)
     greet(groups)
     mine[0] = val[...]
     slot = 0
@@ -437,14 +461,14 @@
 
 
 def count_all(val, zs):
-    n = 1 + 3 + 3 + zs - 1
+    n = 7 + 3 + zs - 1
     return pl.pallas_call(
         functools.partial(count_kernel, zs),
         in_specs=[pl.BlockSpec(memory_space=pltpu.VMEM)],
         out_specs=pl.BlockSpec(memory_space=pltpu.VMEM),
         out_shape=jax.ShapeDtypeStruct(val.shape, F32),
         scratch_shapes=[
-            pltpu.VMEM((5,) + val.shape, F32), pltpu.VMEM((n,) + val.shape, F32),
+            pltpu.VMEM((4,) + val.shape, F32), pltpu.VMEM((n,) + val.shape, F32),
             pltpu.SemaphoreType.DMA((n,)), pltpu.SemaphoreType.DMA((n,)),
         ],
         compiler_params=pltpu.CompilerParams(collective_id=1, has_side_effects=True),
@@ -455,11 +479,12 @@
 def sum_kernel(zs, parts, g1, g2, loss, cnt, o_g1, o_g2, o_loss, val, s1, s2, s3, r1, r2, r3, r4, o0, o1, o2, send, recv):
     c, x, y, z = place()
     cores, xs, ys, zps = groups = ring_peers(zs)
-    feat, hid = o_g1.shape[0], g2.shape[0]
+    feat, hid = o_g1.shape[0], parts * LANES
     first = parts * feat
     for p in range(parts):
         val[pl.ds(p * feat, feat), :] = g1[pl.ds(0, feat), p * LANES:(p + 1) * LANES]
-    val[pl.ds(first, hid), :] = g2[...]
+    for p in range(parts):
+        val[pl.ds(first + p * LANES, LANES), :] = g2[:, p * LANES:(p + 1) * LANES]
     val[pl.ds(first + hid, 8), :] = loss[...]
     spare = val.shape[0] - first - hid - 8
     val[pl.ds(first + hid + 8, spare), :] = jnp.zeros((spare, LANES), F32)
@@ -508,7 +533,8 @@
     run([remote(o1, o0.at[at(c, h)], cores[0])])
     for p in range(parts):
         o_g1[:, p * LANES:(p + 1) * LANES] = o0[pl.ds(p * feat, feat), :]
-    o_g2[...] = o0[pl.ds(first, hid), :]
+    for p in range(parts):
+        o_g2[:, p * LANES:(p + 1) * LANES] = o0[pl.ds(first + p * LANES, LANES), :]
     total = jnp.sum(o0[pl.ds(first + hid, 8), :], axis=0, keepdims=True)
     o_loss[...] = jnp.broadcast_to(-jnp.sum(total, axis=1, keepdims=True) / cnt[0:1, :], o_loss.shape)
 
@@ -516,7 +542,7 @@
 def sum_all(g1, g2, loss, cnt, feat, zs):
     hid = g1.shape[1]
     parts = hid // LANES
-    used = parts * feat + g2.shape[0] + 8
+    used = parts * feat + hid + 8
     rows = used + -used % 512
     h, q, e = rows // 2, rows // 16, rows // 64
     n = 2 * (1 + 6 + 6) + zs - 1
@@ -553,12 +579,12 @@
         list_ok = jnp.arange(lists)[None, :] < send_count[:, None]
         list_rows = jnp.where(list_ok, send_idx, rows).reshape(devs * lists)
         src = edge_src.reshape(rows * deg)
-        wts = jnp.broadcast_to(edge_wt[:, :, None], (rows, deg, LANES)).reshape(rows * deg, LANES)
+        wts = spread_weights(edge_wt.T)
         w1 = jnp.pad(w_one.astype(BF16), ((0, 2 * LANES - feat_in), (0, 0)))
         w2 = jnp.pad(w_two.astype(BF16), ((0, 0), (0, LANES - classes)))
-        own = jnp.pad(feats, ((0, 0), (0, 2 * LANES - feat_in)))
         lab = jnp.where(label_mask == 1, labels, -1)[:, None]
         local_count = jnp.broadcast_to(jnp.sum(label_mask.astype(F32)), (8, LANES))
+        own = jnp.pad(feats, ((0, 0), (0, 2 * LANES - feat_in)))
 
         def exchange(block):
             return lax.all_to_all(block, "graph", 0, 0, tiled=True)
@@ -569,11 +595,12 @@
         halo_two = exchange(pick_rows(list_rows * 2, z_one, lists))
         grad, gw_two, loss_part = layer_two(src * (hid // LANES), wts, z_one, halo_two, w1, w2, lab, cnt, deg, classes)
         agg, halo_grad = scatter_back(src, wts, grad, devs, lists, deg)
+        w2t = jnp.tile(w2.T, (3, 1))
         back = exchange(halo_grad)
-        gw_one = first_grad(list_rows, agg, back, z_one, w1, jnp.tile(w2.T, (3, 1)), lists)
+        gw_one = first_grad(list_rows, agg, back, z_one, w1, w2t, lists)
 
         grad_one, grad_two, loss = sum_all(gw_one, gw_two, loss_part, cnt, feat_in, zs)
-        return loss[0, 0], grad_one, grad_two[:, :classes]
+        return loss[0, 0], grad_one, grad_two[:classes].T
 
     row_spec = P("graph", None)
     vec_spec = P("graph")

time: 268 us -> 251 us (0.937)
  local copies, waits for them, and re-layouts: 33 us -> 17.2 us
  waiting for transfers between devices: 34.2 us -> 24.9 us
  Pallas kernels: 163 us -> 170 us
    broadcast_in_dim x2 -> x0, local copies, waits for them, and re-layouts: 15.8 us -> none  [device_step(): jnp.broadcast_to(edge_wt[:, :, None], (rows, deg, LANES))]
    pallas_call x0 -> x1, Pallas kernels: none -> 11 us  [spread_weights(): pl.pallas_call(spread_kernel, grid=(rows // block,), in_specs=[pl.BlockSp...]
    all_to_all x3, waiting for transfers between devices: 34.2 us -> 24.9 us  [exchange(): return lax.all_to_all(block, 'graph', 0, 0, tiled=True)]
    pallas_call x1, Pallas kernels: 37.3 us -> 34.3 us  [layer_two(): pl.pallas_call(functools.partial(layer_two_kernel, deg, classes), grid=(r...]
    unnamed x35 -> x31, local copies, waits for them, and re-layouts: 7.93 us -> 7.29 us
  transfers between devices with their start and end apart: 3 -> 3, of which waited for: 2 -> 2; matrix products, arithmetic and copies ran while one was open for 4% -> 3% of each run, Pallas kernels for 8% -> 12%
where the time goes in v2:
time: 251 us; the launch traced here: 248 us
  Pallas kernels  170 us (68%)
  starting transfers between devices  31.9 us (13%)
  waiting for transfers between devices  24.9 us (10%)
  local copies, waits for them, and re-layouts  17.2 us (7%)
  other arithmetic  2.66 us (1%)
    pallas_call x1, Pallas kernels, layer_two(): pl.pallas_call(functools.partial(layer_two_kernel, deg, classes), grid=(r...  34.3 us
    all_to_all x3, starting transfers between devices, exchange(): return lax.all_to_all(block, 'graph', 0, 0, tiled=True)  31.9 us
    pallas_call x1, Pallas kernels, sum_all(): pl.pallas_call(functools.partial(sum_kernel, zs, parts), in_specs=[vm] *...  31.4 us
    pallas_call x1, Pallas kernels, scatter_back(): pl.pallas_call(functools.partial(scatter_kernel, deg), grid=(rows // step...  30 us
    all_to_all x3, waiting for transfers between devices, exchange(): return lax.all_to_all(block, 'graph', 0, 0, tiled=True)  24.9 us
    pallas_call x1, Pallas kernels, layer_one(): pl.pallas_call(functools.partial(layer_one_kernel, deg), grid=(rows // st...  24.2 us
    pallas_call x1, Pallas kernels, count_all(): pl.pallas_call(functools.partial(count_kernel, zs), in_specs=[pl.BlockSpe...  19.6 us
    pallas_call x1, Pallas kernels, first_grad(): pl.pallas_call(functools.partial(first_grad_kernel, lists), grid=(1,), in...  12.3 us
  transfers between devices with their start and end apart: 3, of which 2 were waited for; matrix products, arithmetic and copies ran while one was open for 3% of the time, Pallas kernels for 12%

profile of v2, /device:TPU:2, one launch (start us, length us, event | category | flops | bytes accessed | tf_op | source)
XLA Modules:
  0.0 248.1 jit_solution(7833091344314530088)
XLA Ops:
  2.2 3.2 %copy.23 = bf16[4096,200]{1,0:T(8,128)(2,1)S(1)} copy(bf16[4096,200]{0,1:T(8,128)(2,1)} %param.9) | data formatting | bytes 3276800 | tf_op args[0]
  5.4 1.6 pad.12.rows_ref.own
  7.0 3.8 %pick_rows.2 = bf16[256,4,256]{2,1,0:T(4,128)(2,1)} custom-call(s32[1024]{0:T(1024)} %broadcast_multiply_fusion.2.idx, bf16[4096,256]{1,0:T(8,128)(2,1)} %pad.12.rows_ref.own), custom_call_target="tpu_custom_call" | custom-call | tf_op jit(solution)/shard_map/pick_rows/pallas_call | solution.py:83
  10.8 14.7 %all-to-all-start = ((bf16[256,4,256]{2,1,0:T(4,128)(2,1)}), bf16[256,4,256]{2,1,0:T(4,128)(2,1)S(1)}, u32[]{:S(2)}, u32[]{:S(2)}) async-start(bf16[256,4,256]{2,1,0:T(4,128)(2,1)} %pick_rows.2), calls=%async_computation | async-start | bytes 1048576 | tf_op jit(solution)/shard_map/all_to_all | solution.py:590
  25.6 11.0 %spread_weights.1.wts = f32[32768,128]{1,0:T(8,128)} custom-call(f32[8,4096]{1,0:T(8,128)} %bitcast.9), custom_call_target="tpu_custom_call" | custom-call | bytes 16777216 | tf_op jit(solution)/shard_map/spread_weights/pallas_call | solution.py:139
  37.1 1.0 reshape.18.src
  38.9 5.9 %all-to-all-done.halo = bf16[256,4,256]{2,1,0:T(4,128)(2,1)S(1)} async-done(((bf16[256,4,256]{2,1,0:T(4,128)(2,1)}), bf16[256,4,256]{2,1,0:T(4,128)(2,1)S(1)}, u32[]{:S(2)}, u32[]{:S(2)}) %all-to-all-start) | async-done | bytes 524320 | tf_op jit(solution)/shard_map/all_to_all | solution.py:590
  44.7 0.8 copy-done.6
  45.6 24.2 %layer_one.1.rows_ref.own.z_ref = bf16[4096,256]{1,0:T(8,128)(2,1)} custom-call(s32[32768]{0:T(1024)} %get-tuple-element.21.src, f32[32768,128]{1,0:T(8,128)} %spread_weights.1.wts, bf16[4096,256]{1,0:T(8,128)(2,1)} %pad.12.rows_ref.own, bf16[256,4,256]{2,1,0:T(4,128)(2,1)} %copy-done.6), custom_call_target="tpu_custom_call" | custom-call | tf_op jit(solution)/shard_map/layer_one/pallas_call | solution.py:168
  69.8 3.9 %pick_rows.3 = bf16[256,4,256]{2,1,0:T(4,128)(2,1)} custom-call(s32[1024]{0:T(1024)} %broadcast_multiply_fusion.2.idx, bf16[4096,256]{1,0:T(8,128)(2,1)} %layer_one.1.rows_ref.own.z_ref), custom_call_target="tpu_custom_call" | custom-call | tf_op jit(solution)/shard_map/pick_rows/pallas_call | solution.py:83
  73.7 7.9 %all-to-all-start.1 = ((bf16[256,4,256]{2,1,0:T(4,128)(2,1)}), bf16[256,4,256]{2,1,0:T(4,128)(2,1)S(1)}, u32[]{:S(2)}, u32[]{:S(2)}) async-start(bf16[256,4,256]{2,1,0:T(4,128)(2,1)} %pick_rows.3), calls=%async_computation.1 | async-start | bytes 1048576 | tf_op jit(solution)/shard_map/all_to_all | solution.py:590
  83.2 1.2 broadcast_in_dim.19.val
  84.4 19.6 %count_all.1.cnt = f32[8,128]{1,0:T(8,128)} custom-call(f32[8,128]{1,0:T(8,128)} %broadcast_in_dim.19.val), custom_call_target="tpu_custom_call" | custom-call | tf_op jit(solution)/shard_map/count_all/pallas_call | solution.py:465
  104.0 2.0 copy.25.lab
  106.7 0.8 copy-done.4
  107.5 34.3 %layer_two.1 = (f32[4096,128]{1,0:T(8,128)}, f32[128,512]{1,0:T(8,128)}, f32[8,128]{1,0:T(8,128)}) custom-call(s32[32768]{0:T(1024)} %get-tuple-element.22.src, f32[32768,128]{1,0:T(8,128)} %spread_weights.1.wts, bf16[4096,256]{1,0:T(8,128)(2,1)} %layer_one.1.rows_ref.own.z_ref, bf16[256,4,256]{2,1,0:T(4,128)(2,1)} %copy-done.4, bf16[256,512]{1,0:T(8,128)(2,1)} %pad.13.w1, ...), custom_call_target="tpu_custom_call" | custom-call | tf_op jit(solution)/shard_map/layer_two/pallas_call | solution.py:246
  141.9 30.0 %scatter_back.1 = (f32[4096,128]{1,0:T(8,128)}, f32[256,4,128]{2,1,0:T(4,128)}) custom-call(s32[32768]{0:T(1024)} %copy-done.7, f32[32768,128]{1,0:T(8,128)} %spread_weights.1.wts, f32[4096,128]{1,0:T(8,128)} %get-tuple-element.11.grad), custom_call_target="tpu_custom_call" | custom-call | tf_op jit(solution)/shard_map/scatter_back/pallas_call | solution.py:335
  171.9 9.3 %all-to-all-start.2 = ((f32[256,4,128]{2,1,0:T(4,128)}), f32[256,4,128]{2,1,0:T(4,128)S(1)}, u32[]{:S(2)}, u32[]{:S(2)}) async-start(f32[256,4,128]{2,1,0:T(4,128)} %get-tuple-element.13), calls=%async_computation.2 | async-start | bytes 1048576 | tf_op jit(solution)/shard_map/all_to_all | solution.py:590
  181.3 19.1 %all-to-all-done.2.back = f32[256,4,128]{2,1,0:T(4,128)S(1)} async-done(((f32[256,4,128]{2,1,0:T(4,128)}), f32[256,4,128]{2,1,0:T(4,128)S(1)}, u32[]{:S(2)}, u32[]{:S(2)}) %all-to-all-start.2) | async-done | bytes 524320 | tf_op jit(solution)/shard_map/all_to_all | solution.py:590
  200.4 0.8 tile.4
  201.4 12.3 %first_grad.1.g1 = f32[256,512]{1,0:T(8,128)} custom-call(s32[1024]{0:T(1024)} %copy-done.12, f32[4096,128]{1,0:T(8,128)} %get-tuple-element.12.agg, f32[256,4,128]{2,1,0:T(4,128)} %copy-done.5, bf16[4096,256]{1,0:T(8,128)(2,1)} %layer_one.1.rows_ref.own.z_ref, bf16[256,512]{1,0:T(8,128)(2,1)} %pad.13.w1, bf16[384,512]{1,0:T(8,128)(2,1)} %bitcast.8), custom_call_target="tpu_custom_call" | custom-call | tf_op jit(solution)/shard_map/first_grad/pallas_call | solution.py:397
  213.7 1.0 copy-done
  214.7 31.4 %sum_all.1 = (f32[200,512]{1,0:T(8,128)S(1)}, f32[128,512]{1,0:T(8,128)S(1)}, f32[8,128]{1,0:T(8,128)S(1)}) custom-call(f32[256,512]{1,0:T(8,128)S(1)} %copy-done, f32[128,512]{1,0:T(8,128)S(1)} %copy-done.1, f32[8,128]{1,0:T(8,128)S(1)} %copy-done.3, f32[8,128]{1,0:T(8,128)S(1)} %copy-done.2), custom_call_target="tpu_custom_call" | custom-call | tf_op jit(solution)/shard_map/sum_all/pallas_call | solution.py:551
  247.3 0.8 copy.28
  (42 shorter events, 6.6 us)
Async XLA Ops:
  1.6 5.4 %copy-start.12 = (s32[1024]{0:T(1024)}, s32[1024]{0:T(1024)S(1)}, u32[]{:S(2)}) copy-start(s32[1024]{0:T(1024)S(1)} %reshape.17.idx) | copy-start | bytes 12292
  10.8 33.9 %all-to-all-start = ((bf16[256,4,256]{2,1,0:T(4,128)(2,1)}), bf16[256,4,256]{2,1,0:T(4,128)(2,1)S(1)}, u32[]{:S(2)}, u32[]{:S(2)}) async-start(bf16[256,4,256]{2,1,0:T(4,128)(2,1)} %pick_rows.2), calls=%async_computation | async-start | bytes 1048576 | tf_op jit(solution)/shard_map/all_to_all | solution.py:590
  25.5 11.0 %copy-start.10 = (s32[4096,8]{0,1:T(8,128)S(1)}, s32[4096,8]{0,1:T(8,128)}, u32[]{:S(2)}) copy-start(s32[4096,8]{0,1:T(8,128)} %param.14) | copy-start | bytes 393220
  38.2 31.6 %copy-start.7 = (s32[32768]{0:T(1024)}, s32[32768]{0:T(1024)S(1)}, u32[]{:S(2)}) copy-start(s32[32768]{0:T(1024)S(1)} %reshape.18.src) | copy-start | bytes 393220
  44.7 0.8 copy-start.6
  69.7 11.9 %copy-start.9 = (f32[512,107]{0,1:T(8,128)S(1)}, f32[512,107]{0,1:T(8,128)}, u32[]{:S(2)}) copy-start(f32[512,107]{0,1:T(8,128)} %param.11) | copy-start | bytes 657412
  69.8 12.0 %copy-start.8 = (f32[200,512]{1,0:T(8,128)S(1)}, f32[200,512]{1,0:T(8,128)}, u32[]{:S(2)}) copy-start(f32[200,512]{1,0:T(8,128)} %param.10) | copy-start | bytes 1228804
  69.8 12.8 %copy-start.11 = (s32[4096]{0:T(1024)S(1)}, s32[4096]{0:T(1024)}, u32[]{:S(2)}) copy-start(s32[4096]{0:T(1024)} %param.17) | copy-start | bytes 49156
  69.8 34.2 %copy-start.13 = (s32[4096]{0:T(1024)S(1)}, s32[4096]{0:T(1024)}, u32[]{:S(2)}) copy-start(s32[4096]{0:T(1024)} %param.16) | copy-start | bytes 49156
  73.7 33.0 %all-to-all-start.1 = ((bf16[256,4,256]{2,1,0:T(4,128)(2,1)}), bf16[256,4,256]{2,1,0:T(4,128)(2,1)S(1)}, u32[]{:S(2)}, u32[]{:S(2)}) async-start(bf16[256,4,256]{2,1,0:T(4,128)(2,1)} %pick_rows.3), calls=%async_computation.1 | async-start | bytes 1048576 | tf_op jit(solution)/shard_map/all_to_all | solution.py:590
  106.7 0.8 copy-start.4
  171.9 28.5 %all-to-all-start.2 = ((f32[256,4,128]{2,1,0:T(4,128)}), f32[256,4,128]{2,1,0:T(4,128)S(1)}, u32[]{:S(2)}, u32[]{:S(2)}) async-start(f32[256,4,128]{2,1,0:T(4,128)} %get-tuple-element.13), calls=%async_computation.2 | async-start | bytes 1048576 | tf_op jit(solution)/shard_map/all_to_all | solution.py:590
  200.4 0.9 copy-start.5
  201.4 12.3 %copy-start.1 = (f32[128,512]{1,0:T(8,128)S(1)}, f32[128,512]{1,0:T(8,128)}, u32[]{:S(2)}) copy-start(f32[128,512]{1,0:T(8,128)} %get-tuple-element.14.g2) | copy-start | bytes 786436
  201.4 12.3 %copy-start.2 = (f32[8,128]{1,0:T(8,128)S(1)}, f32[8,128]{1,0:T(8,128)}, u32[]{:S(2)}) copy-start(f32[8,128]{1,0:T(8,128)} %count_all.1.cnt) | copy-start | bytes 12292
  201.4 12.3 %copy-start.3 = (f32[8,128]{1,0:T(8,128)S(1)}, f32[8,128]{1,0:T(8,128)}, u32[]{:S(2)}) copy-start(f32[8,128]{1,0:T(8,128)} %get-tuple-element.15.loss) | copy-start | bytes 12292
  213.7 1.0 copy-start
